TPU v7x, 256 devices: a 8x8x2 block of a 8x8x16 slice. The times are simulated.
256 devices in a mesh: rep: 2 (over z), tp: 16 (over y, core), sub: 8 (over x).
Axes of the slice: x: 8, y: 8, z: 2, core: 2. Of those that a mesh axis runs over, the one named last changes fastest.
The devices are a block of a 8x8x16 slice.
Arguments:
- acts: bfloat16 [2048, 16384], P(('rep', 'tp'), 'sub'), parts along dimension 0, may hold values from -6 to 6
- q_src: bfloat16 [32768, 16384], P(('rep', 'sub'), 'tp'), parts along dimension 0, may hold values from -0.046875 to 0.046875
- kv_src: bfloat16 [32768, 2048], P(('rep', 'sub'), 'tp'), parts along dimension 0, may hold values from -0.046875 to 0.046875
- q_src_heads: int32 [128], replicated, may hold values from 0 to 127, as said below
- q_tgt_heads: int32 [128], replicated, may hold values from 0 to 127, as said below
- kv_tgt_heads: int32 [16], replicated, may hold values from 0 to 7, as said below
Outputs:
- q_new: bfloat16 [32768, 16384], P(('rep', 'sub'), 'tp'), parts along dimension 0
- kv_new: bfloat16 [32768, 4096], P(('rep', 'sub'), 'tp'), parts along dimension 0
- qkv: bfloat16 [2048, 20480], P(('rep', 'sub'), 'tp'), parts along dimension 0
There are 2 independent parts, one for each index of `rep`. A program takes and returns all parts, laid end to end along the dimension named above; an argument that names none is the same for every part. Nothing has to cross between parts.
Inputs may be any that keep to these rules, and one draw needn't show every extreme that they name: q_src_heads and q_tgt_heads are permutations. Source block t is entries t * 8 to (t + 1) * 8 - 1 of q_src_heads, target block j the same entries of q_tgt_heads. With s = 4, source block t shares exactly 2 heads with target block (t + min(1, s - 1)) mod 16 and with each target block (t + k * s) mod 16 for k from 1 to 3, and none with any other. `q_tgt_heads`: see q_src_heads. `kv_tgt_heads`: every key-value head appears exactly twice.
All inputs are finite; a program needn't handle non-finite values.
Results may differ from a plain program's by a relative error of at most 0.001.
Values may be sent and summed in bfloat16 or wider, within the bound.
A program may use at most 128 MiB of HBM per device.

v0:
```python
import jax
import jax.numpy as jnp
from jax import lax
from jax.sharding import PartitionSpec as P

HD = 128


def from_behind(block, axis, distance):
    devices = range(lax.axis_size(axis))
    route = [((i - distance) % len(devices), i) for i in devices]
    return lax.ppermute(block, axis, route)


def per_device(acts, q_src, kv_src, q_src_heads, q_tgt_heads, kv_tgt_heads):
    tp_count = lax.axis_size("tp")
    my_index = lax.axis_index("tp")
    row_count = q_src.shape[0]
    q_local = q_src.shape[1] // HD
    capacity = max(2, q_local // tp_count)
    select_count = q_local // capacity
    stride = tp_count // select_count
    head_count = q_src_heads.shape[0]
    head_ids = jnp.arange(head_count, dtype=jnp.int32)
    matches = (q_src_heads[None, :] == q_tgt_heads[:, None]).astype(jnp.int32)
    target_pos = jnp.sum(matches * head_ids[:, None], axis=0)
    slot_of = jnp.sum(matches * head_ids[None, :], axis=1)
    target_dev = target_pos // q_local
    source_dev = head_ids // q_local
    earlier = (
        (source_dev[:, None] == source_dev[None, :])
        & (target_dev[:, None] == target_dev[None, :])
        & (head_ids[None, :] < head_ids[:, None])
    )
    slot_rank = jnp.sum(earlier.astype(jnp.int32), axis=1)
    own_target = lax.dynamic_slice_in_dim(target_dev, my_index * q_local, q_local)
    own_rank = lax.dynamic_slice_in_dim(slot_rank, my_index * q_local, q_local)
    buffer_ids = jnp.arange(tp_count * capacity, dtype=jnp.int32)
    slot_hit = ((own_target * capacity + own_rank)[None, :] == buffer_ids[:, None]).astype(
        jnp.int32
    )
    pick_slot = jnp.sum(slot_hit * jnp.arange(q_local, dtype=jnp.int32)[None, :], axis=1)
    my_slots = lax.dynamic_slice_in_dim(slot_of, my_index * q_local, q_local)
    pick_table = pick_slot.reshape(tp_count, capacity)
    q_three = q_src.reshape(row_count, q_local, HD)
    pieces = []
    for step_number in range(select_count):
        if step_number == 0:
            distance = min(1, stride - 1)
        else:
            distance = step_number * stride
        target_block = (my_index + distance) % tp_count
        chosen_slots = lax.dynamic_index_in_dim(pick_table, target_block, 0, keepdims=False)
        outgoing_piece = jnp.take(q_three, chosen_slots, axis=1)
        outgoing_piece = from_behind(outgoing_piece, "tp", distance)
        pieces.append(outgoing_piece)
    stacked = jnp.concatenate(pieces, axis=1)
    source_block = my_slots // q_local
    offset = (my_index - source_block) % tp_count
    shift_rank = jnp.where(offset % stride == 0, offset // stride, 0)
    compact_ids = shift_rank * capacity + slot_rank[my_slots]
    q_new = jnp.take(stacked, compact_ids, axis=1).reshape(row_count, q_local * HD)
    kv_slots = kv_tgt_heads.shape[0] // tp_count
    kv_whole = lax.all_gather(kv_src, "tp", axis=1, tiled=True)
    own_kv = lax.dynamic_slice_in_dim(kv_tgt_heads, my_index * kv_slots, kv_slots)
    kv_three = kv_whole.reshape(row_count, kv_whole.shape[1] // (2 * HD), 2 * HD)
    kv_new = jnp.take(kv_three, own_kv, axis=1).reshape(row_count, kv_slots * 2 * HD)
    gathered = lax.all_gather(acts, "tp", axis=0, tiled=True)
    joined_cols = jnp.concatenate([q_new, kv_new], axis=1)
    qkv = lax.psum_scatter(
        jnp.dot(gathered, joined_cols, preferred_element_type=jnp.float32),
        "sub",
        scatter_dimension=0,
        tiled=True,
    ).astype(jnp.bfloat16)
    return (q_new, kv_new, qkv)


def solution(mesh):
    in_specs = (
        P(("rep", "tp"), "sub"),
        P(("rep", "sub"), "tp"),
        P(("rep", "sub"), "tp"),
        P(),
        P(),
        P(),
    )
    out_specs = (P(("rep", "sub"), "tp"), P(("rep", "sub"), "tp"), P(("rep", "sub"), "tp"))
    return jax.shard_map(
        per_device, mesh=mesh, in_specs=in_specs, out_specs=out_specs, check_vma=False
    )
```

profile of v0, /device:TPU:513, one launch (start us, length us, event | category | flops | bytes accessed | tf_op | source)
XLA Modules:
  0.0 309.0 jit_solution(1556637233331579625)
XLA Ops:
  7.2 2.0 copy.30
  9.4 0.7 all-gather.5.cloned.1.call-update
  10.3 0.8 fusion.7
  11.1 0.2 convert_reduce_fusion
  11.6 6.4 %copy.24 = bf16[2048,1024]{0,1:T(8,128)(2,1)} copy(bf16[2048,1024]{1,0:T(8,128)(2,1)} %param.9) | data formatting | bytes 8388608 | tf_op args[1]
  18.0 6.5 %copy.25 = bf16[2048,8,128]{2,0,1:T(8,128)(2,1)} copy(bf16[2048,8,128]{0,2,1:T(8,128)(2,1)} %bitcast.43) | data formatting | bytes 8388608 | tf_op jit(solution)/shard_map/reshape | solution.py:45
  24.5 2.9 gather_fusion.2
  27.6 3.9 %collective-permute-start = (bf16[2048,2,128]{2,0,1:T(8,128)(2,1)S(1)}, bf16[2048,2,128]{2,0,1:T(8,128)(2,1)}, u32[]{:S(2)}, u32[]{:S(2)}) collective-permute-start(bf16[2048,2,128]{2,0,1:T(8,128)(2,1)S(1)} %select_bitcast_fusion.3), channel_id=1, source_target_pairs={{120,0},{0,8},{8,16},{16,24},{24,32},{32,40},{40,48},{48,56},{56,6... | collective-permute-start | bytes 3145736 | tf_op jit(solution)/shard_map/ppermute | solution.py:12
  31.5 2.9 gather_fusion.3
  34.6 4.8 %collective-permute-start.1 = (bf16[2048,2,128]{2,0,1:T(8,128)(2,1)S(1)}, bf16[2048,2,128]{2,0,1:T(8,128)(2,1)}, u32[]{:S(2)}, u32[]{:S(2)}) collective-permute-start(bf16[2048,2,128]{2,0,1:T(8,128)(2,1)S(1)} %select_bitcast_fusion.2), channel_id=1, source_target_pairs={{96,0},{104,8},{112,16},{120,24},{0,32},{8,40},{16,48},{24,56},{32... | collective-permute-start | bytes 3145736 | tf_op jit(solution)/shard_map/ppermute | solution.py:12
  39.4 2.9 gather_fusion.4
  42.4 1.1 select_bitcast_fusion.1
  43.5 7.6 %collective-permute-start.2 = (bf16[2048,2,128]{2,0,1:T(8,128)(2,1)}, bf16[2048,2,128]{2,0,1:T(8,128)(2,1)}, u32[]{:S(2)}, u32[]{:S(2)}) collective-permute-start(bf16[2048,2,128]{2,0,1:T(8,128)(2,1)} %select_bitcast_fusion.1), channel_id=1, source_target_pairs={{64,0},{72,8},{80,16},{88,24},{96,32},{104,40},{112,48},{120,56},{... | collective-permute-start | bytes 3145736 | tf_op jit(solution)/shard_map/ppermute | solution.py:12
  51.2 3.0 gather_fusion.5
  54.2 1.1 select_bitcast_fusion
  55.4 0.6 collective-permute-start.3
  56.0 0.6 gather_fusion
  56.7 0.6 dynamic_slice.32
  59.4 103.9 %collective-permute-done.1 = bf16[2048,2,128]{2,0,1:T(8,128)(2,1)} collective-permute-done((bf16[2048,2,128]{2,0,1:T(8,128)(2,1)S(1)}, bf16[2048,2,128]{2,0,1:T(8,128)(2,1)}, u32[]{:S(2)}, u32[]{:S(2)}) %collective-permute-start.1) | collective-permute-done | bytes 1048608 | tf_op jit(solution)/shard_map/ppermute | solution.py:12
  163.3 19.3 %collective-permute-done.2 = bf16[2048,2,128]{2,0,1:T(8,128)(2,1)} collective-permute-done((bf16[2048,2,128]{2,0,1:T(8,128)(2,1)}, bf16[2048,2,128]{2,0,1:T(8,128)(2,1)}, u32[]{:S(2)}, u32[]{:S(2)}) %collective-permute-start.2) | collective-permute-done | bytes 1048608 | tf_op jit(solution)/shard_map/ppermute | solution.py:12
  182.6 3.6 %pad_maximum_fusion = bf16[2048,8,128]{2,0,1:T(8,128)(2,1)} fusion(bf16[2048,2,128]{2,0,1:T(8,128)(2,1)S(1)} %collective-permute-done.3, bf16[2048,2,128]{2,0,1:T(8,128)(2,1)} %collective-permute-done.2, bf16[2048,2,128]{2,0,1:T(8,128)(2,1)} %collective-permute-done.1, bf16[2048,2,128]{2,0,1:T(8,128)(2,1)} %collective-permute-done), kind=kLoop, calls=%fused_computation.11 | loop fusion | flops 6291456 | bytes 8388608 | tf_op jit(solution)/shard_map/concatenate | solution.py:57
  186.2 5.2 %gather_fusion.1 = bf16[8,2048,128]{2,1,0:T(8,128)(2,1)} fusion(bf16[2048,8,128]{2,0,1:T(8,128)(2,1)} %pad_maximum_fusion, s32[1024]{0:T(1024)S(1)} %pad_clamp_fusion), kind=kCustom, calls=%fused_computation.5 | custom fusion | bytes 8388640 | tf_op jit(solution)/shard_map/jit(_take)/gather | solution.py:62
  191.4 6.4 %copy.29 = bf16[2048,8,128]{0,2,1:T(8,128)(2,1)} copy(bf16[2048,8,128]{2,0,1:T(8,128)(2,1)} %bitcast.42) | data formatting | bytes 8388608 | tf_op jit(solution)/shard_map/jit(_take)/gather | solution.py:62
  197.8 4.6 %bitcast_select_fusion = bf16[2048,1024]{0,1:T(8,128)(2,1)} fusion(bf16[2048,8,128]{0,2,1:T(8,128)(2,1)} %copy.29, pred[1024]{0:T(1024)(128)(4,1)S(1)} %broadcast_bitcast_fusion), kind=kLoop, calls=%fused_computation.12 | loop fusion | flops 2097152 | bytes 8389632 | tf_op jit(solution)/shard_map/jit(_take)/select_n | solution.py:62
  202.4 1.4 select_bitcast_fusion.4
  203.8 21.9 %all-gather.5.cloned.1.call-done = bf16[1024,2048]{1,0:T(8,128)(2,1)} async-done(((bf16[64,2048]{1,0:T(8,128)(2,1)}), bf16[1024,2048]{1,0:T(8,128)(2,1)}) %all-gather.5.cloned.1.call-update) | async-done | bytes 4194320 | tf_op jit(solution)/shard_map/all_gather | solution.py:68
  225.7 10.2 %fusion.4 = f32[1024,1280]{0,1:T(8,128)} fusion(bf16[1024,2048]{1,0:T(8,128)(2,1)} %all-gather.5.cloned.1.call-done, bf16[2048,256]{0,1:T(8,128)(2,1)S(1)} %select_bitcast_fusion.4, bf16[2048,1024]{0,1:T(8,128)(2,1)} %bitcast_select_fusion), kind=kOutput, calls=%fused_computation.10 | convolution fusion | flops 5379194880 | bytes 14680064 | tf_op jit(solution)/shard_map/dot_general | solution.py:71
  236.0 6.4 %copy.31 = bf16[2048,1024]{1,0:T(8,128)(2,1)} copy(bf16[2048,1024]{0,1:T(8,128)(2,1)} %bitcast_select_fusion) | data formatting | bytes 8388608
  242.4 1.3 copy.32
  243.7 56.8 %reduce-scatter.2.cloned.1.call-done = f32[128,1280]{0,1:T(8,128)} async-done(((f32[1024,1280]{0,1:T(8,128)}), f32[128,1280]{0,1:T(8,128)}) %reduce-scatter.2.cloned.1.call-update) | async-done | bytes 655376 | tf_op jit(solution)/shard_map/reduce_scatter | solution.py:70
  300.4 1.1 convert_element_type.9
  301.5 0.9 copy.33
  (26 shorter events, 1.2 us)
Async XLA Ops:
  7.2 195.3 %all-gather.3.cloned.1.call-start = ((), (), s32[]{:S(2)}) async-start(), calls=%async_computation.1 | async-start | bytes 8912896 | tf_op jit(solution)/shard_map/all_gather | solution.py:64
  9.3 216.3 %all-gather.5.cloned.1.call-start = ((), (), s32[]{:S(2)}) async-start(), calls=%async_computation.2 | async-start | bytes 4456448 | tf_op jit(solution)/shard_map/all_gather | solution.py:68
  10.2 290.3 %reduce-scatter.2.cloned.1.call-start = ((), (), s32[]{:S(2)}) async-start(), calls=%async_computation.3 | async-start | bytes 5898240 | tf_op jit(solution)/shard_map/reduce_scatter | solution.py:70
  27.6 31.8 %collective-permute-start = (bf16[2048,2,128]{2,0,1:T(8,128)(2,1)S(1)}, bf16[2048,2,128]{2,0,1:T(8,128)(2,1)}, u32[]{:S(2)}, u32[]{:S(2)}) collective-permute-start(bf16[2048,2,128]{2,0,1:T(8,128)(2,1)S(1)} %select_bitcast_fusion.3), channel_id=1, source_target_pairs={{120,0},{0,8},{8,16},{16,24},{24,32},{32,40},{40,48},{48,56},{56,6... | collective-permute-start | bytes 3145736 | tf_op jit(solution)/shard_map/ppermute | solution.py:12
  34.6 128.7 %collective-permute-start.1 = (bf16[2048,2,128]{2,0,1:T(8,128)(2,1)S(1)}, bf16[2048,2,128]{2,0,1:T(8,128)(2,1)}, u32[]{:S(2)}, u32[]{:S(2)}) collective-permute-start(bf16[2048,2,128]{2,0,1:T(8,128)(2,1)S(1)} %select_bitcast_fusion.2), channel_id=1, source_target_pairs={{96,0},{104,8},{112,16},{120,24},{0,32},{8,40},{16,48},{24,56},{32... | collective-permute-start | bytes 3145736 | tf_op jit(solution)/shard_map/ppermute | solution.py:12
  39.4 17.2 %copy-start = (s32[16]{0:T(128)S(1)}, s32[16]{0:T(128)}, u32[]{:S(2)}) copy-start(s32[16]{0:T(128)} %param.13) | copy-start | bytes 196
  43.5 139.0 %collective-permute-start.2 = (bf16[2048,2,128]{2,0,1:T(8,128)(2,1)}, bf16[2048,2,128]{2,0,1:T(8,128)(2,1)}, u32[]{:S(2)}, u32[]{:S(2)}) collective-permute-start(bf16[2048,2,128]{2,0,1:T(8,128)(2,1)} %select_bitcast_fusion.1), channel_id=1, source_target_pairs={{64,0},{72,8},{80,16},{88,24},{96,32},{104,40},{112,48},{120,56},{... | collective-permute-start | bytes 3145736 | tf_op jit(solution)/shard_map/ppermute | solution.py:12
  55.4 127.2 %collective-permute-start.3 = (bf16[2048,2,128]{2,0,1:T(8,128)(2,1)}, bf16[2048,2,128]{2,0,1:T(8,128)(2,1)S(1)}, u32[]{:S(2)}, u32[]{:S(2)}) collective-permute-start(bf16[2048,2,128]{2,0,1:T(8,128)(2,1)} %select_bitcast_fusion), channel_id=1, source_target_pairs={{32,0},{40,8},{48,16},{56,24},{64,32},{72,40},{80,48},{88,56},{96,... | collective-permute-start | bytes 3145736 | tf_op jit(solution)/shard_map/ppermute | solution.py:12
Sparse Core Ops, SparseCore 0:
  9.9 152.4 all-gather.2
  164.2 61.4 all-gather.4
  236.1 64.2 reduce-scatter.1
where the time goes:
time: 310 us; the launch traced here: 309 us
  waiting for transfers between devices  203 us (65%)
  local copies, waits for them, and re-layouts  48.4 us (16%)
  starting transfers between devices  17.1 us (6%)
  between operations  15.9 us (5%)
  other arithmetic  14.7 us (5%)
  matrix products  10.2 us (3%)
    ppermute x4, waiting for transfers between devices, from_behind(): return lax.ppermute(block, axis, route)  123 us
    reduce_scatter x1, waiting for transfers between devices, per_device(): lax.psum_scatter(jnp.dot(gathered, joined_cols, preferred_element_type=jn...  56.8 us
    all_gather x1, waiting for transfers between devices, per_device(): gathered = lax.all_gather(acts, 'tp', axis=0, tiled=True)  21.9 us
    unnamed x7, local copies, waits for them, and re-layouts  17.1 us
    ppermute x4, starting transfers between devices, from_behind(): return lax.ppermute(block, axis, route)  16.9 us
    gather x4, local copies, waits for them, and re-layouts, per_device(): outgoing_piece = jnp.take(q_three, chosen_slots, axis=1)  11.8 us
    gather x2, local copies, waits for them, and re-layouts, per_device(): jnp.take(stacked, compact_ids, axis=1).reshape(row_count, q_local * HD)  11.6 us
    dot_general x1, matrix products, per_device(): jnp.dot(gathered, joined_cols, preferred_element_type=jnp.float32)  10.2 us
  transfers between devices with their start and end apart: 7, of which 4 were waited for; matrix products, arithmetic and copies ran while one was open for 19% of the time, Pallas kernels for 0%

commit v1 on v0

--- a/solution.py
+++ b/solution.py
@@ -65,7 +65,9 @@
     own_kv = lax.dynamic_slice_in_dim(kv_tgt_heads, my_index * kv_slots, kv_slots)
     kv_three = kv_whole.reshape(row_count, kv_whole.shape[1] // (2 * HD), 2 * HD)
     kv_new = jnp.take(kv_three, own_kv, axis=1).reshape(row_count, kv_slots * 2 * HD)
-    gathered = lax.all_gather(acts, "tp", axis=0, tiled=True)
+    gathered = jnp.concatenate(
+        lax.all_to_all(jnp.stack([acts] * lax.axis_size("tp")), "tp", 0, 0), axis=0
+    )
     joined_cols = jnp.concatenate([q_new, kv_new], axis=1)
     qkv = lax.psum_scatter(
         jnp.dot(gathered, joined_cols, preferred_element_type=jnp.float32),

time: 310 us -> 378 us (1.22)
  waiting for transfers between devices: 203 us -> 250 us
  starting transfers between devices: 17.1 us -> 34.8 us
    ppermute x4, waiting for transfers between devices: 123 us -> 196 us  [from_behind(): return lax.ppermute(block, axis, route)]
    all_to_all x0 -> x1, starting transfers between devices: none -> 24.8 us  [per_device(): lax.all_to_all(jnp.stack([acts] * lax.axis_size('tp')), 'tp', 0, 0)]
    all_gather x1 -> x0, waiting for transfers between devices: 21.9 us -> none  [per_device(): gathered = lax.all_gather(acts, 'tp', axis=0, tiled=True)]
    ppermute x4, starting transfers between devices: 16.9 us -> 9.8 us  [from_behind(): return lax.ppermute(block, axis, route)]
    unnamed x7 -> x11, local copies, waits for them, and re-layouts: 17.1 us -> 17.1 us
  transfers between devices with their start and end apart: 7 -> 7, of which waited for: 4 -> 4; matrix products, arithmetic and copies ran while one was open for 19% -> 16% of each run, Pallas kernels for 0% -> 0%
where the time goes in v1:
time: 378 us; the launch traced here: 377 us
  waiting for transfers between devices  250 us (66%)
  local copies, waits for them, and re-layouts  51.8 us (14%)
  starting transfers between devices  34.8 us (9%)
  between operations  16.2 us (4%)
  other arithmetic  14 us (4%)
  matrix products  10.2 us (3%)
    ppermute x4, waiting for transfers between devices, from_behind(): return lax.ppermute(block, axis, route)  196 us
    reduce_scatter x1, waiting for transfers between devices, per_device(): lax.psum_scatter(jnp.dot(gathered, joined_cols, preferred_element_type=jn...  54.4 us
    all_to_all x1, starting transfers between devices, per_device(): lax.all_to_all(jnp.stack([acts] * lax.axis_size('tp')), 'tp', 0, 0)  24.8 us
    unnamed x11, local copies, waits for them, and re-layouts  17.1 us
    gather x4, local copies, waits for them, and re-layouts, per_device(): outgoing_piece = jnp.take(q_three, chosen_slots, axis=1)  11.8 us
    gather x2, local copies, waits for them, and re-layouts, per_device(): jnp.take(stacked, compact_ids, axis=1).reshape(row_count, q_local * HD)  11.6 us
    dot_general x1, matrix products, per_device(): jnp.dot(gathered, joined_cols, preferred_element_type=jnp.float32)  10.2 us
    ppermute x4, starting transfers between devices, from_behind(): return lax.ppermute(block, axis, route)  9.8 us
  transfers between devices with their start and end apart: 7, of which 4 were waited for; matrix products, arithmetic and copies ran while one was open for 16% of the time, Pallas kernels for 0%

profile of v1, /device:TPU:513, one launch (start us, length us, event | category | flops | bytes accessed | tf_op | source)
XLA Modules:
  0.0 377.0 jit_solution(16363120815594065839)
XLA Ops:
  7.2 2.0 copy.30
  9.3 3.4 stack.2
  12.7 24.8 %all-to-all-start = ((bf16[16,64,2048]{2,1,0:T(8,128)(2,1)}), bf16[16,64,2048]{2,1,0:T(8,128)(2,1)}, u32[]{:S(2)}, u32[]{:S(2)}) async-start(bf16[16,64,2048]{2,1,0:T(8,128)(2,1)} %stack.2), calls=%async_computation | async-start | bytes 8388608 | tf_op jit(solution)/shard_map/all_to_all | solution.py:69
  37.9 0.2 convert_reduce_fusion
  38.4 6.4 %copy.24 = bf16[2048,1024]{0,1:T(8,128)(2,1)} copy(bf16[2048,1024]{1,0:T(8,128)(2,1)} %param.9) | data formatting | bytes 8388608 | tf_op args[1]
  44.8 6.5 %copy.25 = bf16[2048,8,128]{2,0,1:T(8,128)(2,1)} copy(bf16[2048,8,128]{0,2,1:T(8,128)(2,1)} %bitcast.44) | data formatting | bytes 8388608 | tf_op jit(solution)/shard_map/reshape | solution.py:45
  51.3 2.9 gather_fusion.2
  54.4 1.7 collective-permute-start
  56.1 2.9 gather_fusion.3
  59.2 2.3 collective-permute-start.1
  61.5 2.9 gather_fusion.4
  64.5 1.1 select_bitcast_fusion.1
  65.6 2.6 collective-permute-start.2
  68.2 3.0 gather_fusion.5
  71.2 1.1 select_bitcast_fusion
  72.3 3.2 collective-permute-start.3
  75.6 0.6 gather_fusion
  76.3 0.6 dynamic_slice.32
  79.0 119.8 %collective-permute-done = bf16[2048,2,128]{2,0,1:T(8,128)(2,1)} collective-permute-done((bf16[2048,2,128]{2,0,1:T(8,128)(2,1)S(1)}, bf16[2048,2,128]{2,0,1:T(8,128)(2,1)}, u32[]{:S(2)}, u32[]{:S(2)}) %collective-permute-start) | collective-permute-done | bytes 1048608 | tf_op jit(solution)/shard_map/ppermute | solution.py:12
  198.9 50.1 %collective-permute-done.1 = bf16[2048,2,128]{2,0,1:T(8,128)(2,1)} collective-permute-done((bf16[2048,2,128]{2,0,1:T(8,128)(2,1)S(1)}, bf16[2048,2,128]{2,0,1:T(8,128)(2,1)}, u32[]{:S(2)}, u32[]{:S(2)}) %collective-permute-start.1) | collective-permute-done | bytes 1048608 | tf_op jit(solution)/shard_map/ppermute | solution.py:12
  248.9 25.7 %collective-permute-done.2 = bf16[2048,2,128]{2,0,1:T(8,128)(2,1)} collective-permute-done((bf16[2048,2,128]{2,0,1:T(8,128)(2,1)}, bf16[2048,2,128]{2,0,1:T(8,128)(2,1)}, u32[]{:S(2)}, u32[]{:S(2)}) %collective-permute-start.2) | collective-permute-done | bytes 1048608 | tf_op jit(solution)/shard_map/ppermute | solution.py:12
  274.6 3.6 pad_maximum_fusion
  278.2 5.2 %gather_fusion.1 = bf16[8,2048,128]{2,1,0:T(8,128)(2,1)} fusion(bf16[2048,8,128]{2,0,1:T(8,128)(2,1)} %pad_maximum_fusion, s32[1024]{0:T(1024)S(1)} %pad_clamp_fusion), kind=kCustom, calls=%fused_computation.5 | custom fusion | bytes 8388640 | tf_op jit(solution)/shard_map/jit(_take)/gather | solution.py:62
  283.4 6.4 %copy.29 = bf16[2048,8,128]{0,2,1:T(8,128)(2,1)} copy(bf16[2048,8,128]{2,0,1:T(8,128)(2,1)} %bitcast.43) | data formatting | bytes 8388608 | tf_op jit(solution)/shard_map/jit(_take)/gather | solution.py:62
  289.9 4.6 %bitcast_select_fusion = bf16[2048,1024]{0,1:T(8,128)(2,1)} fusion(bf16[2048,8,128]{0,2,1:T(8,128)(2,1)} %copy.29, pred[1024]{0:T(1024)(128)(4,1)S(1)} %broadcast_bitcast_fusion), kind=kLoop, calls=%fused_computation.12 | loop fusion | flops 2097152 | bytes 8389632 | tf_op jit(solution)/shard_map/jit(_take)/select_n | solution.py:62
  294.4 1.3 select_bitcast_fusion.4
  295.8 10.2 %fusion.4 = f32[1024,1280]{0,1:T(8,128)} fusion(bf16[1024,2048]{1,0:T(8,128)(2,1)} %bitcast.16, bf16[2048,256]{0,1:T(8,128)(2,1)S(1)} %select_bitcast_fusion.4, bf16[2048,1024]{0,1:T(8,128)(2,1)} %bitcast_select_fusion), kind=kOutput, calls=%fused_computation.10 | convolution fusion | flops 5379194880 | bytes 14680064 | tf_op jit(solution)/shard_map/dot_general | solution.py:73
  306.0 6.4 %copy.31 = bf16[2048,1024]{1,0:T(8,128)(2,1)} copy(bf16[2048,1024]{0,1:T(8,128)(2,1)} %bitcast_select_fusion) | data formatting | bytes 8388608
  312.4 1.3 copy.32
  313.7 54.4 %reduce-scatter.2.cloned.1.call-done = f32[128,1280]{0,1:T(8,128)} async-done(((f32[1024,1280]{0,1:T(8,128)}), f32[128,1280]{0,1:T(8,128)}) %reduce-scatter.2.cloned.1.call-update) | async-done | bytes 655376 | tf_op jit(solution)/shard_map/reduce_scatter | solution.py:72
  368.1 1.1 convert_element_type.9
  369.3 0.9 copy.33
  (30 shorter events, 1.3 us)
Async XLA Ops:
  7.2 287.3 %all-gather.2.cloned.1.call-start = ((), (), s32[]{:S(2)}) async-start(), calls=%async_computation.2 | async-start | bytes 8912896 | tf_op jit(solution)/shard_map/all_gather | solution.py:64
  12.7 25.0 %copy-start = (s32[128]{0:T(128)S(1)}, s32[128]{0:T(128)}, u32[]{:S(2)}) copy-start(s32[128]{0:T(128)} %param.11) | copy-start | bytes 1540
  12.7 25.0 %copy-start.1 = (s32[128]{0:T(128)S(1)}, s32[128]{0:T(128)}, u32[]{:S(2)}) copy-start(s32[128]{0:T(128)} %param.12) | copy-start | bytes 1540
  12.7 283.0 %all-to-all-start = ((bf16[16,64,2048]{2,1,0:T(8,128)(2,1)}), bf16[16,64,2048]{2,1,0:T(8,128)(2,1)}, u32[]{:S(2)}, u32[]{:S(2)}) async-start(bf16[16,64,2048]{2,1,0:T(8,128)(2,1)} %stack.2), calls=%async_computation | async-start | bytes 8388608 | tf_op jit(solution)/shard_map/all_to_all | solution.py:69
  37.6 330.6 %reduce-scatter.2.cloned.1.call-start = ((), (), s32[]{:S(2)}) async-start(), calls=%async_computation.3 | async-start | bytes 5898240 | tf_op jit(solution)/shard_map/reduce_scatter | solution.py:72
  54.4 144.4 %collective-permute-start = (bf16[2048,2,128]{2,0,1:T(8,128)(2,1)S(1)}, bf16[2048,2,128]{2,0,1:T(8,128)(2,1)}, u32[]{:S(2)}, u32[]{:S(2)}) collective-permute-start(bf16[2048,2,128]{2,0,1:T(8,128)(2,1)S(1)} %select_bitcast_fusion.3), channel_id=1, source_target_pairs={{120,0},{0,8},{8,16},{16,24},{24,32},{32,40},{40,48},{48,56},{56,6... | collective-permute-start | bytes 3145736 | tf_op jit(solution)/shard_map/ppermute | solution.py:12
  59.2 189.7 %collective-permute-start.1 = (bf16[2048,2,128]{2,0,1:T(8,128)(2,1)S(1)}, bf16[2048,2,128]{2,0,1:T(8,128)(2,1)}, u32[]{:S(2)}, u32[]{:S(2)}) collective-permute-start(bf16[2048,2,128]{2,0,1:T(8,128)(2,1)S(1)} %select_bitcast_fusion.2), channel_id=1, source_target_pairs={{96,0},{104,8},{112,16},{120,24},{0,32},{8,40},{16,48},{24,56},{32... | collective-permute-start | bytes 3145736 | tf_op jit(solution)/shard_map/ppermute | solution.py:12
  61.5 14.8 %copy-start.2 = (s32[16]{0:T(128)S(1)}, s32[16]{0:T(128)}, u32[]{:S(2)}) copy-start(s32[16]{0:T(128)} %param.13) | copy-start | bytes 196
  65.6 209.0 %collective-permute-start.2 = (bf16[2048,2,128]{2,0,1:T(8,128)(2,1)}, bf16[2048,2,128]{2,0,1:T(8,128)(2,1)}, u32[]{:S(2)}, u32[]{:S(2)}) collective-permute-start(bf16[2048,2,128]{2,0,1:T(8,128)(2,1)} %select_bitcast_fusion.1), channel_id=1, source_target_pairs={{64,0},{72,8},{80,16},{88,24},{96,32},{104,40},{112,48},{120,56},{... | collective-permute-start | bytes 3145736 | tf_op jit(solution)/shard_map/ppermute | solution.py:12
  72.3 202.3 %collective-permute-start.3 = (bf16[2048,2,128]{2,0,1:T(8,128)(2,1)}, bf16[2048,2,128]{2,0,1:T(8,128)(2,1)S(1)}, u32[]{:S(2)}, u32[]{:S(2)}) collective-permute-start(bf16[2048,2,128]{2,0,1:T(8,128)(2,1)} %select_bitcast_fusion), channel_id=1, source_target_pairs={{32,0},{40,8},{48,16},{56,24},{64,32},{72,40},{80,48},{88,56},{96,... | collective-permute-start | bytes 3145736 | tf_op jit(solution)/shard_map/ppermute | solution.py:12
Sparse Core Ops, SparseCore 0:
  9.9 173.4 all-gather.1
  306.2 61.9 reduce-scatter.1
